TPU v7x, 256 devices: a whole 4x4x8 slice. The times are simulated.
256 devices in a mesh: grp: 4 (over y), dev: 64 (over x, z, core).
Axes of the slice: x: 4, y: 4, z: 8, core: 2. Of those that a mesh axis runs over, the one named last changes fastest.
Arguments:
- pool_rows: bfloat16 [262144, 1024], P(('grp', 'dev')), may hold values from -6 to 6
- sample_index: int32 [262144], P(('grp', 'dev')), may hold values from 0 to 262143, as said below
- cluster_id: int32 [262144], P(('grp', 'dev')), may hold values from 0 to 511, as said below
- child_id: int32 [262144], P(('grp', 'dev')), may hold values from 0 to 7
- old_centroids: float32 [512, 8, 1024], P('dev'), may hold values from -6 to 6
Outputs:
- centroids: float32 [512, 8, 1024], P('dev')
- child_counts: int32 [512, 8], P('dev')
Inputs may be any that keep to these rules, and one draw needn't show every extreme that they name: Sample i takes a pool row of its own aligned block of 1024 rows: sample_index[i] // 1024 == i // 1024. `cluster_id`: in each aligned block of 1024 samples (the rows of one device) the 2 clusters o * 2 to o * 2 + 1 of any owner o are named at most 8 times together, and one cluster, the same in every block, is named exactly 8 times in every block.
All inputs are finite; a program needn't handle non-finite values.
Results may differ from a plain program's by a relative error of at most 0.0003.
Values may be sent and summed in bfloat16 or wider, within the bound.
A program may use at most 64 MiB of HBM per device.

v0:
```python
import math

import jax
import jax.numpy as jnp
from jax import lax
from jax.sharding import PartitionSpec as P


def side_by_side(arrays, axis, dim, along):
    widths = [math.prod(a.shape[along:]) for a in arrays]
    both = jnp.concatenate(
        [a.reshape(*a.shape[:along], w) for a, w in zip(arrays, widths)], axis=along
    )
    filled = lax.all_gather(both, axis, axis=dim, tiled=True)
    parts = jnp.split(filled, [sum(widths[:k]) for k in range(1, len(widths))], axis=along)
    return tuple(
        (b.reshape(*filled.shape[:along], *a.shape[along:]) for a, b in zip(arrays, parts))
    )


def segment_totals(rows, segment, segments):
    onehot = (jnp.arange(segments, dtype=jnp.int32)[:, None] == segment[None, :]).astype(
        jnp.bfloat16
    )
    sums = jnp.dot(onehot, rows, preferred_element_type=jnp.float32)
    counts = jnp.sum(onehot.astype(jnp.float32), axis=1)
    return (sums, counts)


def rank_within(keys_here):
    positions = jnp.arange(keys_here.shape[0], dtype=jnp.int32)
    matches = keys_here[:, None] == keys_here[None, :]
    earlier = positions[None, :] < positions[:, None]
    return jnp.sum(matches & earlier, axis=1)


def per_device(pool_rows, sample_index, cluster_id, child_id, old_centroids):
    rows_dev, row_width = pool_rows.shape
    block_clusters, kinds = (old_centroids.shape[0], old_centroids.shape[1])
    groups = lax.axis_size("grp")
    owners = lax.axis_size("dev")
    owned = block_clusters // groups
    clusters = block_clusters * owners
    most = 4 * rows_dev // clusters
    sample = pool_rows[sample_index % rows_dev]
    holder_table = cluster_id // owned
    slot_of = holder_table * most + rank_within(holder_table)
    total_slots = clusters // owned * most
    label_of = cluster_id % owned * kinds + child_id
    buffer = jnp.zeros((total_slots, row_width), jnp.bfloat16).at[slot_of].set(sample)
    labels = jnp.full((total_slots,), -1, jnp.int32).at[slot_of].set(label_of)
    shaped = buffer.reshape(owners, groups, most, row_width)
    shaped_labels = labels.reshape(owners, groups, most)
    arrived, arrived_labels = (
        lax.all_to_all(
            lax.all_to_all(shaped, "dev", split_axis=0, concat_axis=0, tiled=True),
            "grp",
            split_axis=1,
            concat_axis=1,
            tiled=True,
        ),
        lax.all_to_all(
            lax.all_to_all(shaped_labels, "dev", split_axis=0, concat_axis=0, tiled=True),
            "grp",
            split_axis=1,
            concat_axis=1,
            tiled=True,
        ),
    )
    sums, counts = segment_totals(
        arrived.reshape(-1, row_width), arrived_labels.reshape(-1), owned * kinds
    )
    group_index = lax.axis_index("grp")
    mine = lax.dynamic_slice_in_dim(old_centroids, group_index * owned, owned, 0)
    counts_owned = counts.reshape(owned, kinds)
    fresh = (sums.reshape(owned, kinds, row_width) + mine) / (counts_owned[:, :, None] + 1.0)
    centroids, new_counts = side_by_side((fresh, counts_owned), "grp", 0, 2)
    return (centroids, new_counts.astype(jnp.int32))


def solution(mesh):
    placed = (
        P(("grp", "dev"), None),
        P(("grp", "dev")),
        P(("grp", "dev")),
        P(("grp", "dev")),
        P("dev", None, None),
    )
    return jax.shard_map(
        per_device,
        mesh=mesh,
        in_specs=placed,
        out_specs=(P("dev", None, None), P("dev", None)),
        check_vma=False,
    )
```

profile of v0, /device:TPU:1, one launch (start us, length us, event | category | flops | bytes accessed | tf_op | source)
XLA Modules:
  0.0 220.0 jit_solution(11543515831146436987)
XLA Ops:
  0.6 0.8 add_select_fusion.2
  1.5 0.5 convert_reduce_fusion
  2.0 0.7 fusion.10
  2.8 4.3 %scatter_custom_fusion = s32[2048]{0:T(1024)S(1)} fusion(s32[1024]{0:T(1024)S(1)} %get-tuple-element.3, s32[1024]{0:T(1024)S(1)} %get-tuple-element.2, s32[]{:T(128)} %constant.47.clone.1), kind=kCustom, calls=%fused_computation.34 | custom fusion | bytes 8196 | tf_op jit(solution)/shard_map/scatter | solution.py:51
  7.1 0.8 reshape.46
  7.9 13.0 %all-to-all-start = ((s32[64,4,8]{2,1,0:T(4,128)}), s32[64,4,8]{2,1,0:T(4,128)S(1)}, u32[]{:S(2)}, u32[]{:S(2)}) async-start(s32[64,4,8]{2,1,0:T(4,128)} %reshape.46), calls=%async_computation | async-start | bytes 262144 | tf_op jit(solution)/shard_map/all_to_all | solution.py:63
  20.9 15.3 %scatter_custom_fusion.1 = bf16[2048,1024]{1,0:T(8,128)(2,1)} fusion(s32[1024]{0:T(1024)S(1)} %get-tuple-element.3, bf16[1024,1024]{1,0:T(8,128)(2,1)S(1)} %copy-done, s32[1024]{0:T(1024)S(1)} %get-tuple-element.4, bf16[]{:T(256)} %constant.52.clone.1), kind=kCustom, calls=%fused_computation.6 | custom fusion | bytes 4194306 | tf_op jit(solution)/shard_map/scatter | solution.py:50
  36.2 10.5 %all-to-all-start.2 = ((bf16[64,4,8,1024]{3,2,1,0:T(8,128)(2,1)}), bf16[64,4,8,1024]{3,2,1,0:T(8,128)(2,1)}, u32[]{:S(2)}, u32[]{:S(2)}) async-start(bf16[64,4,8,1024]{3,2,1,0:T(8,128)(2,1)} %bitcast.10), calls=%async_computation.2 | async-start | bytes 8388608 | tf_op jit(solution)/shard_map/all_to_all | solution.py:56
  46.8 0.7 reshape.85
  47.5 95.1 %all-to-all-done.2 = bf16[64,4,8,1024]{3,2,1,0:T(8,128)(2,1)} async-done(((bf16[64,4,8,1024]{3,2,1,0:T(8,128)(2,1)}), bf16[64,4,8,1024]{3,2,1,0:T(8,128)(2,1)}, u32[]{:S(2)}, u32[]{:S(2)}) %all-to-all-start.2) | async-done | bytes 4194336 | tf_op jit(solution)/shard_map/all_to_all | solution.py:56
  142.6 4.2 %all-to-all-start.1 = ((s32[4,1,512]{2,1,0:T(1,128)}), s32[4,1,512]{2,1,0:T(1,128)S(1)}, u32[]{:S(2)}, u32[]{:S(2)}) async-start(s32[4,1,512]{2,1,0:T(1,128)} %reshape.85), calls=%async_computation.1 | async-start | bytes 16384 | tf_op jit(solution)/shard_map/all_to_all | solution.py:62
  146.8 4.8 %copy.22 = bf16[64,4,8,1024]{3,2,0,1:T(8,128)(2,1)} copy(bf16[64,4,8,1024]{3,2,1,0:T(8,128)(2,1)} %all-to-all-done.2) | data formatting | bytes 8388608 | tf_op jit(solution)/shard_map/all_to_all | solution.py:56
  151.5 4.9 %all-to-all-start.3 = ((bf16[64,4,8,1024]{3,2,0,1:T(8,128)(2,1)}), bf16[64,4,8,1024]{3,2,0,1:T(8,128)(2,1)}, u32[]{:S(2)}, u32[]{:S(2)}) async-start(bf16[64,4,8,1024]{3,2,0,1:T(8,128)(2,1)} %copy.22), calls=%async_computation.3 | async-start | bytes 8388608 | tf_op jit(solution)/shard_map/all_to_all | solution.py:55
  156.4 0.5 broadcast.69
  156.9 0.7 reduce
  157.8 0.2 eq.55
  158.0 0.1 convert_reduce_fusion.1
  158.3 46.0 %all-to-all-done.3 = bf16[64,4,8,1024]{3,2,0,1:T(8,128)(2,1)} async-done(((bf16[64,4,8,1024]{3,2,0,1:T(8,128)(2,1)}), bf16[64,4,8,1024]{3,2,0,1:T(8,128)(2,1)}, u32[]{:S(2)}, u32[]{:S(2)}) %all-to-all-start.3) | async-done | bytes 4194336 | tf_op jit(solution)/shard_map/all_to_all | solution.py:55
  204.3 2.6 %copy.23 = bf16[64,4,8,1024]{3,2,1,0:T(8,128)(2,1)S(1)} copy(bf16[64,4,8,1024]{3,2,0,1:T(8,128)(2,1)} %all-to-all-done.3) | data formatting | bytes 8388608 | tf_op jit(solution)/shard_map/all_to_all | solution.py:55
  206.9 1.5 fusion.4
  208.5 10.1 %all_gather.3 = f32[8,8,1025]{2,1,0:T(8,128)S(1)} all-gather(f32[2,8,1025]{2,1,0:T(8,128)S(1)} %pad_maximum_fusion), channel_id=1, replica_groups=mesh['grp'=4,'dev'=64] {'grp'}, dimensions={0}, use_global_device_ids=true | all-gather | bytes 328000 | tf_op jit(solution)/shard_map/all_gather | solution.py:14
  218.6 0.7 split.8
  219.3 0.1 copy.26
  219.4 0.6 convert_bitcast_fusion
  (13 shorter events, 0.5 us)
Async XLA Ops:
  0.6 20.3 %copy-start = (bf16[1024,1024]{1,0:T(8,128)(2,1)S(1)}, bf16[1024,1024]{1,0:T(8,128)(2,1)}, u32[]{:S(2)}) copy-start(bf16[1024,1024]{1,0:T(8,128)(2,1)} %param.5) | copy-start | bytes 6291460
  7.9 28.3 %all-to-all-start = ((s32[64,4,8]{2,1,0:T(4,128)}), s32[64,4,8]{2,1,0:T(4,128)S(1)}, u32[]{:S(2)}, u32[]{:S(2)}) async-start(s32[64,4,8]{2,1,0:T(4,128)} %reshape.46), calls=%async_computation | async-start | bytes 262144 | tf_op jit(solution)/shard_map/all_to_all | solution.py:63
  36.2 106.4 %all-to-all-start.2 = ((bf16[64,4,8,1024]{3,2,1,0:T(8,128)(2,1)}), bf16[64,4,8,1024]{3,2,1,0:T(8,128)(2,1)}, u32[]{:S(2)}, u32[]{:S(2)}) async-start(bf16[64,4,8,1024]{3,2,1,0:T(8,128)(2,1)} %bitcast.10), calls=%async_computation.2 | async-start | bytes 8388608 | tf_op jit(solution)/shard_map/all_to_all | solution.py:56
  142.6 8.9 %all-to-all-start.1 = ((s32[4,1,512]{2,1,0:T(1,128)}), s32[4,1,512]{2,1,0:T(1,128)S(1)}, u32[]{:S(2)}, u32[]{:S(2)}) async-start(s32[4,1,512]{2,1,0:T(1,128)} %reshape.85), calls=%async_computation.1 | async-start | bytes 16384 | tf_op jit(solution)/shard_map/all_to_all | solution.py:62
  151.5 52.7 %all-to-all-start.3 = ((bf16[64,4,8,1024]{3,2,0,1:T(8,128)(2,1)}), bf16[64,4,8,1024]{3,2,0,1:T(8,128)(2,1)}, u32[]{:S(2)}, u32[]{:S(2)}) async-start(bf16[64,4,8,1024]{3,2,0,1:T(8,128)(2,1)} %copy.22), calls=%async_computation.3 | async-start | bytes 8388608 | tf_op jit(solution)/shard_map/all_to_all | solution.py:55
where the time goes:
time: 223 us; the launch traced here: 220 us
  waiting for transfers between devices  141 us (63%)
  starting transfers between devices  32.5 us (15%)
  local copies, waits for them, and re-layouts  30.5 us (14%)
  blocking collectives  10.1 us (5%)
  other arithmetic  3.54 us (2%)
    all_to_all x1, waiting for transfers between devices, per_device(): lax.all_to_all(shaped, 'dev', split_axis=0, concat_axis=0, tiled=True)  95.1 us
    all_to_all x1, waiting for transfers between devices, per_device(): lax.all_to_all(lax.all_to_all(shaped, 'dev', split_axis=0, concat_axis=0,...  46 us
    scatter x1, local copies, waits for them, and re-layouts, per_device(): jnp.zeros((total_slots, row_width), jnp.bfloat16).at[slot_of].set(sample)  15.3 us
    all_to_all x1, starting transfers between devices, per_device(): lax.all_to_all(shaped_labels, 'dev', split_axis=0, concat_axis=0, tiled=T...  13 us
    all_to_all x1, starting transfers between devices, per_device(): lax.all_to_all(shaped, 'dev', split_axis=0, concat_axis=0, tiled=True)  10.5 us
    all_gather x1, blocking collectives, side_by_side(): filled = lax.all_gather(both, axis, axis=dim, tiled=True)  10.1 us
    all_to_all x1, starting transfers between devices, per_device(): lax.all_to_all(lax.all_to_all(shaped, 'dev', split_axis=0, concat_axis=0,...  4.86 us
    all_to_all x1, local copies, waits for them, and re-layouts, per_device(): lax.all_to_all(shaped, 'dev', split_axis=0, concat_axis=0, tiled=True)  4.75 us
  transfers between devices with their start and end apart: 4, of which 2 were waited for; matrix products, arithmetic and copies ran while one was open for 10% of the time, Pallas kernels for 0%

commit v1 on v0

v1 whole, which is shorter than its diff:
```python
import functools

import jax
import jax.numpy as jnp
from jax import lax
from jax.experimental import pallas as pl
from jax.experimental.pallas import tpu as pltpu
from jax.sharding import PartitionSpec as P

MESH = pl.DeviceIdType.MESH
F32, BF16, I32 = jnp.float32, jnp.bfloat16, jnp.int32

NY, NX, NZ, NC = 4, 4, 8, 2
MEMBERS, SLOTS = 8, 32
BLOCK = MEMBERS * SLOTS
ROWS, WIDTH = 1024, 1024
HALF = WIDTH // 2
SEGS = 64
OWN = 16
AHEAD = 3


def kernel(
    pool_ref, index_ref, cluster_ref, child_ref, old_ref,
    out_ref, count_ref,
    slot_ref, values_ref, send, recv, lab_send, lab_recv,
    z_send, z_recv, total, part_recv, fresh,
    c_send, c_recv, c_mid, c_mid_recv, c_last, c_last_recv,
    data_ss, data_rs, lab_ss, lab_rs, z_ss, z_rs, part_ss, part_rs,
    gather_ss, gather_rs, c_ss, c_rs, own_sem,
):
    y = lax.axis_index("grp")
    d = lax.axis_index("dev")
    x, z, c = d // (NZ * NC), (d // NC) % NZ, d % NC

    def dev(x_, z_, c_):
        return (x_ * NZ + z_) * NC + c_

    def member(h, r):
        e = ((x if h == 0 else y) * NC + c + r) % MEMBERS
        if h == 0:
            return (y, dev(e // NC, z, e % NC))
        return (e // NC, dev(x, z, e % NC))

    def along_z(step):
        return (y, dev(x, (z + step + NZ) % NZ, c))

    def other(h, i):
        if h == 0:
            return ((y + i) % NY, d)
        return (y, dev((x + i) % NX, z, c))

    def push(src, dst, ss, rs, to):
        pltpu.make_async_remote_copy(
            src_ref=src, dst_ref=dst, send_sem=ss, recv_sem=rs, device_id=to, device_id_type=MESH
        ).start()

    def await_bytes(ref, sem):
        pltpu.make_async_copy(ref, ref, sem).wait()

    barrier = pltpu.get_barrier_semaphore()
    greeted = [member(h, r) for h in (0, 1) for r in range(1, MEMBERS)]
    greeted += [along_z(s) for s in range(1, NZ)]
    for to in greeted:
        pl.semaphore_signal(barrier, inc=1, device_id=to, device_id_type=MESH)

    cluster, child = cluster_ref[...], child_ref[...]
    index = index_ref[...] & (ROWS - 1)
    cx, cz, cc, cj = cluster >> 7, (cluster >> 4) & 7, (cluster >> 3) & 1, cluster & 7
    zr = (cz - z + NZ) & (NZ - 1)
    pos = jnp.where(zr >= 4, 2 * (zr - 4), 7 - 2 * zr)
    rx = (cx * NC + cc - (x * NC + c) + MEMBERS) & (MEMBERS - 1)
    ry = ((cj >> 1) * NC + cc - (y * NC + c) + MEMBERS) & (MEMBERS - 1)
    label_x = cj * 8 + child
    label_y = cx * OWN + (cj & 1) * 8 + child
    cat_x = pos * MEMBERS + rx
    cat_y = pos * MEMBERS + ry + 64

    sub = lax.broadcasted_iota(I32, (128, 128), 0)
    lane = lax.broadcasted_iota(I32, (128, 128), 1)
    before = jnp.concatenate(
        [jnp.where(sub <= lane, 1.0, 0.0), jnp.ones((128, 128), F32)], axis=1
    ).astype(BF16)
    hits = []
    for b in range(ROWS // 128):
        at = slice(b * 128, (b + 1) * 128)
        hits.append((sub == cat_x[:, at]) | (sub == cat_y[:, at]))
    stacked = jnp.concatenate([jnp.where(m, 1.0, 0.0).astype(BF16) for m in hits], axis=0)
    ranks = jnp.dot(stacked, before, preferred_element_type=F32)
    base = ((sub & 63) * SLOTS - 1).astype(F32)
    for b in range(ROWS // 128):
        at = slice(b * 128, (b + 1) * 128)
        here = ranks[b * 128 : (b + 1) * 128]
        chosen = jnp.where(hits[b], here[:, :128] + base, 0.0)
        slot_ref[0, :, at] = jnp.sum(chosen[:64], axis=0, keepdims=True).astype(I32)
        slot_ref[1, :, at] = jnp.sum(chosen[64:], axis=0, keepdims=True).astype(I32)
        base = base + here[:, 128:]

    values = jnp.concatenate(
        [index >> 5, index & 31, label_x + 1, label_y + 1, jnp.zeros((4, ROWS), I32)], axis=0
    ).astype(F32)
    values = jnp.concatenate([values, jnp.zeros((120, ROWS), F32)], axis=0)
    values_ref[...] = values.T.astype(BF16)

    sub_block = lax.broadcasted_iota(I32, (BLOCK, ROWS), 0)
    lane_block = lax.broadcasted_iota(I32, (BLOCK, ROWS), 1)
    lab_lane = lax.broadcasted_iota(I32, (1, BLOCK), 1)

    def place(p, h):
        pick = jnp.where(sub_block == slot_ref[h] - p * BLOCK, 1.0, 0.0).astype(BF16)
        found = jnp.dot(pick, values_ref[...], preferred_element_type=F32)
        row = (found[:, 0:1] * 32.0 + found[:, 1:2]).astype(I32)
        labels = found.T[2 + h : 3 + h].astype(I32)
        take = jnp.where(lane_block == row, 1.0, 0.0).astype(BF16)
        rows = jnp.dot(
            take, pool_ref[:, h * HALF : (h + 1) * HALF], preferred_element_type=F32
        ).astype(BF16)
        recv[h, p, 0] = rows[:SLOTS]
        send[h, p, pl.ds(1, MEMBERS - 1)] = rows[SLOTS:].reshape(MEMBERS - 1, SLOTS, HALF)
        for r in range(MEMBERS):
            mine = jnp.where((lab_lane >> 5) == r, labels, 0)
            if r == 0:
                lab_recv[h, p, 0] = mine
            else:
                lab_send[h, p, r] = mine

    def dispatch(p, h):
        for r in range(1, MEMBERS):
            to = member(h, r)
            push(lab_send.at[h, p, r], lab_recv.at[h, p, r], lab_ss.at[h, p], lab_rs.at[h, p], to)
            push(send.at[h, p, r], recv.at[h, p, r], data_ss.at[h, p], data_rs.at[h, p], to)

    seg = lax.broadcasted_iota(I32, (SEGS, BLOCK), 0) + 1

    def reduce_rows(p, h):
        await_bytes(lab_recv.at[h, p, pl.ds(1, MEMBERS - 1)], lab_rs.at[h, p])
        await_bytes(recv.at[h, p, pl.ds(1, MEMBERS - 1)], data_rs.at[h, p])
        labels = lab_recv[h, p, 0]
        for r in range(1, MEMBERS):
            labels = labels + lab_recv[h, p, r]
        onehot = jnp.where(seg == labels, 1.0, 0.0).astype(BF16)
        return jnp.dot(onehot, recv[h, p].reshape(BLOCK, HALF), preferred_element_type=F32)

    UP, DOWN = 0, 1

    def forward(h, way, k, partial):
        z_send[h, way, k] = partial
        to = along_z(1 if way == UP else -1)
        push(z_send.at[h, way, k], z_recv.at[h, way, k], z_ss.at[h, way, k], z_rs.at[h, way, k], to)

    def incoming(h, way, k):
        await_bytes(z_recv.at[h, way, k], z_rs.at[h, way, k])
        return z_recv[h, way, k]

    pl.semaphore_wait(barrier, len(greeted))

    def first(p, carry):
        for h in (0, 1):
            place(p, h)
            dispatch(p, h)
        return carry

    lax.fori_loop(0, AHEAD, first, 0)

    place_row = rx * NZ + cz
    a_hot = jnp.where(lax.broadcasted_iota(I32, (64, ROWS), 0) == place_row, 1.0, 0.0).astype(BF16)
    b_hot = jnp.where(lax.broadcasted_iota(I32, (128, ROWS), 0) == label_x, 1.0, 0.0).astype(BF16)
    tally = lax.dot_general(a_hot, b_hot, (((1,), (1,)), ((), ())), preferred_element_type=F32)
    c_send[...] = tally.reshape(MEMBERS, NZ, 128)
    for r in range(1, MEMBERS):
        push(c_send.at[r], c_recv.at[r], c_ss.at[0], c_rs.at[0], member(0, r))

    forward(0, UP, 3, reduce_rows(0, 0))
    forward(1, DOWN, 3, reduce_rows(0, 1))

    await_bytes(c_recv.at[pl.ds(1, MEMBERS - 1)], c_rs.at[0])
    group_count = c_send[0]
    for r in range(1, MEMBERS):
        group_count = group_count + c_recv[r]
    c_mid[...] = group_count
    for s in range(1, NZ):
        push(c_mid, c_mid_recv.at[s], c_ss.at[1], c_rs.at[1], along_z(s))

    def pair(i, carry):
        k = 2 - i
        for way in (UP, DOWN):
            p = 1 + 2 * i + way
            for h in (0, 1):
                partial = reduce_rows(p, h)
                if way == h:
                    partial = partial + incoming(h, way, k + 1)
                else:
                    z_send[h, way, k] = partial

                    @pl.when(i > 0)
                    def _():
                        z_send[h, way, k] += incoming(h, way, k + 1)

                    partial = None
                if partial is not None:
                    z_send[h, way, k] = partial
                to = along_z(1 if way == UP else -1)
                push(z_send.at[h, way, k], z_recv.at[h, way, k], z_ss.at[h, way, k], z_rs.at[h, way, k], to)

            @pl.when(p + AHEAD - 1 < 8)
            def _():
                first(p + AHEAD - 1, 0)

        return carry

    lax.fori_loop(0, 3, pair, 0)

    await_bytes(c_mid_recv.at[pl.ds(1, NZ - 1)], c_rs.at[1])
    plane_count = c_mid[...]
    for s in range(1, NZ):
        plane_count = plane_count + c_mid_recv[s]
    c_last[...] = plane_count
    for i in range(1, NY):
        push(c_last, c_last_recv.at[i], c_ss.at[2], c_rs.at[2], other(0, i))

    for h in (0, 1):
        own = reduce_rows(7, h)
        own = own + incoming(h, UP, 0)
        own = own + incoming(h, DOWN, 0)
        total[h] = own.reshape(4, OWN, HALF)
        at = y if h == 0 else x
        for i in range(1, 4):
            push(total.at[h, (at + i) % 4], part_recv.at[h, i], part_ss.at[h], part_rs.at[h], other(h, i))

    await_bytes(c_last_recv.at[pl.ds(1, NY - 1)], c_rs.at[2])
    all_count = c_last[...]
    for i in range(1, NY):
        all_count = all_count + c_last_recv[i]
    row_of = lax.broadcasted_iota(I32, (NZ, 128), 0)
    block_count = jnp.sum(jnp.where(row_of == z, all_count, 0.0), axis=0, keepdims=True)
    for j in range(8):
        count_ref[j : j + 1, :] = block_count[:, j * 8 : (j + 1) * 8].astype(I32)
    own_sub = lax.broadcasted_iota(I32, (OWN, 128), 0) + y * OWN
    own_lane = lax.broadcasted_iota(I32, (OWN, 128), 1)
    column = jnp.sum(jnp.where(own_sub == own_lane, block_count, 0.0), axis=1, keepdims=True)

    for h in (0, 1):
        at = y if h == 0 else x
        cols = pl.ds(h * HALF, HALF)
        await_bytes(part_recv.at[h, pl.ds(1, 3)], part_rs.at[h])
        mine = total[h, at]
        for i in range(1, 4):
            mine = mine + part_recv[h, i]
        old = old_ref[pl.ds(y * 2, 2), :, cols].reshape(OWN, HALF)
        fresh[:, :, cols] = ((mine + old) / (column + 1.0)).reshape(2, 8, HALF)
        src = fresh.at[:, :, cols]
        dst = out_ref.at[pl.ds(y * 2, 2), :, cols]
        for i in range(1, NY):
            push(src, dst, gather_ss.at[h], gather_rs.at[h], other(0, i))
        pltpu.make_async_copy(src, dst, own_sem.at[h]).start()

    for h in (0, 1):
        for p in range(8):
            await_bytes(lab_send.at[h, p, pl.ds(1, MEMBERS - 1)], lab_ss.at[h, p])
            await_bytes(send.at[h, p, pl.ds(1, MEMBERS - 1)], data_ss.at[h, p])
        for way in (UP, DOWN):
            for k in range(4 if way == h else 3):
                await_bytes(z_send.at[h, way, k], z_ss.at[h, way, k])
        await_bytes(part_recv.at[h, pl.ds(1, 3)], part_ss.at[h])
        cols = pl.ds(h * HALF, HALF)
        await_bytes(out_ref.at[pl.ds(0, 6), :, cols], gather_ss.at[h])
        await_bytes(out_ref.at[pl.ds(0, 6), :, cols], gather_rs.at[h])
        await_bytes(out_ref.at[pl.ds(0, 2), :, cols], own_sem.at[h])
    await_bytes(c_recv.at[pl.ds(1, MEMBERS - 1)], c_ss.at[0])
    await_bytes(c_mid_recv.at[pl.ds(1, NZ - 1)], c_ss.at[1])
    await_bytes(c_last_recv.at[pl.ds(1, NY - 1)], c_ss.at[2])


def per_device(pool_rows, sample_index, cluster_id, child_id, old_centroids):
    vmem = pl.BlockSpec(memory_space=pltpu.VMEM)
    dma = pltpu.SemaphoreType.DMA
    centroids, counts = pl.pallas_call(
        kernel,
        out_shape=(
            jax.ShapeDtypeStruct((8, 8, WIDTH), F32),
            jax.ShapeDtypeStruct((8, 8), I32),
        ),
        in_specs=[vmem] * 5,
        out_specs=(pl.BlockSpec(memory_space=pl.ANY), vmem),
        scratch_shapes=[
            pltpu.VMEM((2, 1, ROWS), I32),
            pltpu.VMEM((ROWS, 128), BF16),
            pltpu.VMEM((2, 8, MEMBERS, SLOTS, HALF), BF16),
            pltpu.VMEM((2, 8, MEMBERS, SLOTS, HALF), BF16),
            pltpu.VMEM((2, 8, MEMBERS, 1, BLOCK), I32),
            pltpu.VMEM((2, 8, MEMBERS, 1, BLOCK), I32),
            pltpu.VMEM((2, 2, 4, SEGS, HALF), F32),
            pltpu.VMEM((2, 2, 4, SEGS, HALF), F32),
            pltpu.VMEM((2, 4, OWN, HALF), F32),
            pltpu.VMEM((2, 4, OWN, HALF), F32),
            pltpu.VMEM((2, 8, WIDTH), F32),
            pltpu.VMEM((MEMBERS, NZ, 128), F32),
            pltpu.VMEM((MEMBERS, NZ, 128), F32),
            pltpu.VMEM((NZ, 128), F32),
            pltpu.VMEM((NZ, NZ, 128), F32),
            pltpu.VMEM((NZ, 128), F32),
            pltpu.VMEM((NY, NZ, 128), F32),
            dma((2, 8)), dma((2, 8)), dma((2, 8)), dma((2, 8)),
            dma((2, 2, 4)), dma((2, 2, 4)), dma((2,)), dma((2,)),
            dma((2,)), dma((2,)), dma((3,)), dma((3,)), dma((2,)),
        ],
        compiler_params=pltpu.CompilerParams(
            collective_id=0, has_side_effects=True, vmem_limit_bytes=48 << 20
        ),
    )(
        pool_rows,
        sample_index.reshape(1, ROWS),
        cluster_id.reshape(1, ROWS),
        child_id.reshape(1, ROWS),
        old_centroids,
    )
    return centroids, counts


def solution(mesh):
    placed = (
        P(("grp", "dev"), None),
        P(("grp", "dev")),
        P(("grp", "dev")),
        P(("grp", "dev")),
        P("dev", None, None),
    )
    return jax.shard_map(
        per_device,
        mesh=mesh,
        in_specs=placed,
        out_specs=(P("dev", None, None), P("dev", None)),
        check_vma=False,
    )
```

time: 223 us -> 62.9 us (0.28); the launches traced: 220 us -> 62.6 us
  waiting for transfers between devices: 141 us -> 0 us
  Pallas kernels: 0 us -> 56.1 us
  starting transfers between devices: 32.5 us -> 0 us
  local copies, waits for them, and re-layouts: 30.5 us -> 5.89 us
  blocking collectives: 10.1 us -> 0 us
  other arithmetic: 3.54 us -> 0 us
    all_to_all x4 -> x0, waiting for transfers between devices: 141 us -> none  [the longest x1 95.1 us: per_device(): lax.all_to_all(shaped, 'dev', split_axis=0, concat_axis=0, tiled=True)]
    pallas_call x0 -> x1, Pallas kernels: none -> 56.1 us  [per_device(): pl.pallas_call(kernel, out_shape=(jax.ShapeDtypeStruct((8, 8, WIDTH), F32...]
    all_to_all x4 -> x0, starting transfers between devices: 32.5 us -> none  [the longest x1 13 us: per_device(): lax.all_to_all(shaped_labels, 'dev', split_axis=0, concat_axis=0, tiled=T...]
    scatter x2 -> x0, local copies, waits for them, and re-layouts: 19.6 us -> none  [the longest x1 15.3 us: per_device(): jnp.zeros((total_slots, row_width), jnp.bfloat16).at[slot_of].set(sample)]
    all_gather x1 -> x0, blocking collectives: 10.1 us -> none  [side_by_side(): filled = lax.all_gather(both, axis, axis=dim, tiled=True)]
    all_to_all x5 -> x0, local copies, waits for them, and re-layouts: 8.08 us -> none  [the longest x1 4.75 us: per_device(): lax.all_to_all(shaped, 'dev', split_axis=0, concat_axis=0, tiled=True)]
    unnamed x5 -> x12, local copies, waits for them, and re-layouts: 0.9 us -> 5.89 us
  transfers between devices with their start and end apart: 4 -> 0, of which waited for: 2 -> 0; matrix products, arithmetic and copies ran while one was open for 10% -> 0% of each run, Pallas kernels for 0% -> 0%
where the time goes in v1:
time: 62.9 us; the launch traced here: 62.6 us
  Pallas kernels  56.1 us (89%)
  local copies, waits for them, and re-layouts  5.89 us (9%)
  between operations  0.65 us (1%)
    pallas_call x1, Pallas kernels, per_device(): pl.pallas_call(kernel, out_shape=(jax.ShapeDtypeStruct((8, 8, WIDTH), F32...  56.1 us
    unnamed x12, local copies, waits for them, and re-layouts  5.89 us

profile of v1, /device:TPU:1, one launch (start us, length us, event | category | flops | bytes accessed | tf_op | source)
XLA Modules:
  0.0 62.6 jit_solution(13065070145842518584)
XLA Ops:
  0.6 0.0 copy-start
  0.6 1.6 %copy-done = bf16[1024,1024]{1,0:T(8,128)(2,1)S(1)} copy-done((bf16[1024,1024]{1,0:T(8,128)(2,1)S(1)}, bf16[1024,1024]{1,0:T(8,128)(2,1)}, u32[]{:S(2)}) %copy-start) | copy-done | bytes 2097176
  2.2 0.0 copy-start.1
  2.2 0.9 %copy-done.1 = f32[8,8,1024]{2,1,0:T(8,128)S(1)} copy-done((f32[8,8,1024]{2,1,0:T(8,128)S(1)}, f32[8,8,1024]{2,1,0:T(8,128)}, u32[]{:S(2)}) %copy-start.1) | copy-done | bytes 262168
  3.2 0.0 copy-start.2
  3.2 0.7 %copy-done.2 = s32[1024]{0:T(1024)S(1)} copy-done((s32[1024]{0:T(1024)S(1)}, s32[1024]{0:T(1024)}, u32[]{:S(2)}) %copy-start.2) | copy-done | bytes 4120
  3.9 0.0 copy-start.3
  3.9 0.7 %copy-done.3 = s32[1024]{0:T(1024)S(1)} copy-done((s32[1024]{0:T(1024)S(1)}, s32[1024]{0:T(1024)}, u32[]{:S(2)}) %copy-start.3) | copy-done | bytes 4120
  4.5 0.0 copy-start.4
  4.6 0.7 %copy-done.4 = s32[1024]{0:T(1024)S(1)} copy-done((s32[1024]{0:T(1024)S(1)}, s32[1024]{0:T(1024)}, u32[]{:S(2)}) %copy-start.4) | copy-done | bytes 4120
  5.2 56.1 %shard_map.68 = (f32[8,8,1024]{2,1,0:T(8,128)S(1)}, s32[8,8]{1,0:T(8,128)S(1)}) custom-call(bf16[1024,1024]{1,0:T(8,128)(2,1)S(1)} %copy-done, s32[1,1024]{1,0:T(1,128)S(1)} %bitcast.3, s32[1,1024]{1,0:T(1,128)S(1)} %bitcast.4, s32[1,1024]{1,0:T(1,128)S(1)} %bitcast.5, f32[8,8,1024]{2,1,0:T(8,128)S(1)} %copy-done.1), custom_call_target="tpu_custom_call" | custom-call | tf_op jit(solution)/shard_map/pallas_call | solution.py:277
  61.3 0.7 %copy.9 = f32[8,8,1024]{2,1,0:T(8,128)} copy(f32[8,8,1024]{2,1,0:T(8,128)S(1)} %get-tuple-element.4) | data formatting | bytes 524288
  62.0 0.6 copy.10
Async XLA Ops:
  0.6 1.6 %copy-start = (bf16[1024,1024]{1,0:T(8,128)(2,1)S(1)}, bf16[1024,1024]{1,0:T(8,128)(2,1)}, u32[]{:S(2)}) copy-start(bf16[1024,1024]{1,0:T(8,128)(2,1)} %pool_ref.1) | copy-start | bytes 6291460
  2.2 0.9 %copy-start.1 = (f32[8,8,1024]{2,1,0:T(8,128)S(1)}, f32[8,8,1024]{2,1,0:T(8,128)}, u32[]{:S(2)}) copy-start(f32[8,8,1024]{2,1,0:T(8,128)} %old_ref.1) | copy-start | bytes 786436
  3.2 0.7 %copy-start.2 = (s32[1024]{0:T(1024)S(1)}, s32[1024]{0:T(1024)}, u32[]{:S(2)}) copy-start(s32[1024]{0:T(1024)} %param.6) | copy-start | bytes 12292
  3.9 0.7 %copy-start.3 = (s32[1024]{0:T(1024)S(1)}, s32[1024]{0:T(1024)}, u32[]{:S(2)}) copy-start(s32[1024]{0:T(1024)} %param.7) | copy-start | bytes 12292
  4.5 0.7 %copy-start.4 = (s32[1024]{0:T(1024)S(1)}, s32[1024]{0:T(1024)}, u32[]{:S(2)}) copy-start(s32[1024]{0:T(1024)} %param.8) | copy-start | bytes 12292

commit v2 on v1

v2 whole, which is shorter than its diff:
```python
import jax
import jax.numpy as jnp
from jax import lax
from jax.experimental import pallas as pl
from jax.experimental.pallas import tpu as pltpu
from jax.sharding import PartitionSpec as P

MESH = pl.DeviceIdType.MESH
F32, BF16, I32 = jnp.float32, jnp.bfloat16, jnp.int32

NY, NX, NZ, NC = 4, 4, 8, 2
MEMBERS, SLOTS = 8, 32
BLOCK = MEMBERS * SLOTS
ROWS, WIDTH = 1024, 1024
HALF = WIDTH // 2
SEGS = 64
OWN = 16
AHEAD = 3
PIECES = 2
PIECE = HALF // PIECES
LATE = 6


def kernel(
    pool_hbm, index_hbm, cluster_hbm, child_hbm, old_hbm,
    out_ref, count_ref,
    pool_ref, index_ref, cluster_ref, child_ref, old_ref,
    slot_ref, values_ref, send, recv, lab_send, lab_recv,
    z_send, z_recv, total, part_recv, fresh,
    c_send, c_recv, c_group, cz_send, cz_recv, c_last, c_last_recv,
    in_sem, data_ss, data_rs, lab_ss, lab_rs, z_ss, z_rs, part_ss, part_rs,
    gather_ss, gather_rs, c_ss, c_rs, cz_ss, cz_rs, own_sem, late_ss, late_rs, last_ss, last_rs,
):
    y = lax.axis_index("grp")
    d = lax.axis_index("dev")
    x, z, c = d // (NZ * NC), (d // NC) % NZ, d % NC

    def dev(x_, z_, c_):
        return (x_ * NZ + z_) * NC + c_

    def member(h, r):
        e = ((x if h == 0 else y) * NC + c + r) % MEMBERS
        if h == 0:
            return (y, dev(e // NC, z, e % NC))
        return (e // NC, dev(x, z, e % NC))

    def along_z(step):
        return (y, dev(x, (z + step + NZ) % NZ, c))

    def other(h, i):
        if h == 0:
            return ((y + i) % NY, d)
        return (y, dev((x + i) % NX, z, c))

    def push(src, dst, ss, rs, to):
        pltpu.make_async_remote_copy(
            src_ref=src, dst_ref=dst, send_sem=ss, recv_sem=rs, device_id=to, device_id_type=MESH
        ).start()

    def await_bytes(ref, sem):
        pltpu.make_async_copy(ref, ref, sem).wait()

    inputs = [
        pltpu.make_async_copy(src, dst, in_sem.at[i])
        for i, (src, dst) in enumerate(
            [(index_hbm, index_ref), (cluster_hbm, cluster_ref), (child_hbm, child_ref),
             (pool_hbm, pool_ref), (old_hbm, old_ref)]
        )
    ]
    for copy in inputs:
        copy.start()

    barrier = pltpu.get_barrier_semaphore()
    greeted = [member(h, r) for h in (0, 1) for r in range(1, MEMBERS)]
    greeted += [along_z(1), along_z(-1)]
    for to in greeted:
        pl.semaphore_signal(barrier, inc=1, device_id=to, device_id_type=MESH)

    for copy in inputs[:3]:
        copy.wait()
    cluster, child = cluster_ref[...], child_ref[...]
    index = index_ref[...] & (ROWS - 1)
    cx, cz, cc, cj = cluster >> 7, (cluster >> 4) & 7, (cluster >> 3) & 1, cluster & 7
    zr = (cz - z + NZ) & (NZ - 1)
    pos_x = jnp.where(zr >= 4, 2 * (zr - 4), 7 - 2 * zr)
    zr = (NZ - zr) & (NZ - 1)
    pos_y = jnp.where(zr >= 4, 2 * (zr - 4), 7 - 2 * zr)
    rx = (cx * NC + cc - (x * NC + c) + MEMBERS) & (MEMBERS - 1)
    ry = ((cj >> 1) * NC + cc - (y * NC + c) + MEMBERS) & (MEMBERS - 1)
    label_x = cj * 8 + child
    label_y = cx * OWN + (cj & 1) * 8 + child
    cat_x = pos_x * MEMBERS + rx
    cat_y = pos_y * MEMBERS + ry + 64

    sub = lax.broadcasted_iota(I32, (128, 128), 0)
    lane = lax.broadcasted_iota(I32, (128, 128), 1)
    before = jnp.concatenate(
        [jnp.where(sub <= lane, 1.0, 0.0), jnp.ones((128, 128), F32)], axis=1
    ).astype(BF16)
    hits = []
    for b in range(ROWS // 128):
        at = slice(b * 128, (b + 1) * 128)
        hits.append((sub == cat_x[:, at]) | (sub == cat_y[:, at]))
    stacked = jnp.concatenate([jnp.where(m, 1.0, 0.0).astype(BF16) for m in hits], axis=0)
    ranks = jnp.dot(stacked, before, preferred_element_type=F32)
    base = ((sub & 63) * SLOTS - 1).astype(F32)
    for b in range(ROWS // 128):
        at = slice(b * 128, (b + 1) * 128)
        here = ranks[b * 128 : (b + 1) * 128]
        chosen = jnp.where(hits[b], here[:, :128] + base, 0.0)
        slot_ref[0, :, at] = jnp.sum(chosen[:64], axis=0, keepdims=True).astype(I32)
        slot_ref[1, :, at] = jnp.sum(chosen[64:], axis=0, keepdims=True).astype(I32)
        base = base + here[:, 128:]

    values = jnp.concatenate(
        [index >> 5, index & 31, label_x + 1, label_y + 1, jnp.zeros((4, ROWS), I32)], axis=0
    ).astype(F32)
    values = jnp.concatenate([values, jnp.zeros((120, ROWS), F32)], axis=0)
    values_ref[...] = values.T.astype(BF16)

    sub_block = lax.broadcasted_iota(I32, (BLOCK, ROWS), 0)
    lane_block = lax.broadcasted_iota(I32, (BLOCK, ROWS), 1)
    lab_lane = lax.broadcasted_iota(I32, (1, BLOCK), 1)

    def place(p, h):
        pick = jnp.where(sub_block == slot_ref[h] - p * BLOCK, 1.0, 0.0).astype(BF16)
        found = jnp.dot(pick, values_ref[...], preferred_element_type=F32)
        row = (found[:, 0:1] * 32.0 + found[:, 1:2]).astype(I32)
        labels = found.T[2 + h : 3 + h].astype(I32)
        take = jnp.where(lane_block == row, 1.0, 0.0).astype(BF16)
        rows = jnp.dot(
            take, pool_ref[:, h * HALF : (h + 1) * HALF], preferred_element_type=F32
        ).astype(BF16)
        recv[h, p, 0] = rows[:SLOTS]
        send[h, p, pl.ds(1, MEMBERS - 1)] = rows[SLOTS:].reshape(MEMBERS - 1, SLOTS, HALF)
        for r in range(MEMBERS):
            mine = jnp.where((lab_lane >> 5) == r, labels, 0)
            if r == 0:
                lab_recv[h, p, 0] = mine
            else:
                lab_send[h, p, r] = mine

    def columns(q):
        return pl.ds(q * PIECE, PIECE)

    def dispatch(p, h):
        for r in range(1, MEMBERS):
            to = member(h, r)
            push(lab_send.at[h, p, r], lab_recv.at[h, p, r], lab_ss.at[h, p], lab_rs.at[h, p], to)
            push(send.at[h, p, r], recv.at[h, p, r], data_ss.at[h, p], data_rs.at[h, p], to)

    def dispatch_pieces(p, h):
        for q in range(PIECES):
            for r in range(1, MEMBERS):
                to = member(h, r)
                if q == 0:
                    push(lab_send.at[h, p, r], lab_recv.at[h, p, r], lab_ss.at[h, p], lab_rs.at[h, p], to)
                at = (h, p - LATE, q)
                push(
                    send.at[h, p, r, :, columns(q)], recv.at[h, p, r, :, columns(q)],
                    late_ss.at[at], late_rs.at[at], to,
                )

    seg = lax.broadcasted_iota(I32, (SEGS, BLOCK), 0) + 1

    def onehot_of(p, h):
        await_bytes(lab_recv.at[h, p, pl.ds(1, MEMBERS - 1)], lab_rs.at[h, p])
        labels = lab_recv[h, p, 0]
        for r in range(1, MEMBERS):
            labels = labels + lab_recv[h, p, r]
        return jnp.where(seg == labels, 1.0, 0.0).astype(BF16)

    def reduce_rows(p, h):
        onehot = onehot_of(p, h)
        await_bytes(recv.at[h, p, pl.ds(1, MEMBERS - 1)], data_rs.at[h, p])
        return jnp.dot(onehot, recv[h, p].reshape(BLOCK, HALF), preferred_element_type=F32)

    def reduce_piece(onehot, p, h, q):
        await_bytes(recv.at[h, p, pl.ds(1, MEMBERS - 1), :, columns(q)], late_rs.at[h, p - LATE, q])
        rows = recv[h, p, :, :, columns(q)].reshape(BLOCK, PIECE)
        return jnp.dot(onehot, rows, preferred_element_type=F32)

    def onward(h, way):
        return along_z(1 if way == h else -1)

    def forward(h, way, k):
        push(
            z_send.at[h, way, k], z_recv.at[h, way, k], z_ss.at[h, way, k], z_rs.at[h, way, k],
            onward(h, way),
        )

    def incoming(h, way, k):
        await_bytes(z_recv.at[h, way, k], z_rs.at[h, way, k])
        return z_recv[h, way, k]

    def forward_count(way, k):
        push(
            cz_send.at[way, k], cz_recv.at[way, k], cz_ss.at[way, k], cz_rs.at[way, k],
            onward(0, way),
        )

    def incoming_count(way, k):
        await_bytes(cz_recv.at[way, k], cz_rs.at[way, k])
        return cz_recv[way, k]

    def count_of(steps):
        return c_group[pl.ds((z + steps + NZ) % NZ, 1), :]

    def first(p, carry):
        for h in (0, 1):
            place(p, h)

            @pl.when(p < LATE)
            def _():
                dispatch(p, h)

            @pl.when(p >= LATE)
            def _():
                dispatch_pieces(p, h)

        return carry

    def opening(p, carry):
        for h in (0, 1):
            place(p, h)
            dispatch(p, h)
        return carry

    inputs[3].wait()
    pl.semaphore_wait(barrier, len(greeted))
    lax.fori_loop(0, 1, opening, 0)

    place_row = rx * NZ + cz
    a_hot = jnp.where(lax.broadcasted_iota(I32, (64, ROWS), 0) == place_row, 1.0, 0.0).astype(BF16)
    b_hot = jnp.where(lax.broadcasted_iota(I32, (128, ROWS), 0) == label_x, 1.0, 0.0).astype(BF16)
    tally = lax.dot_general(a_hot, b_hot, (((1,), (1,)), ((), ())), preferred_element_type=F32)
    c_send[...] = tally.reshape(MEMBERS, NZ, 128)
    for r in range(1, MEMBERS):
        push(c_send.at[r], c_recv.at[r], c_ss.at[0], c_rs.at[0], member(0, r))

    lax.fori_loop(1, AHEAD, opening, 0)

    await_bytes(c_recv.at[pl.ds(1, MEMBERS - 1)], c_rs.at[0])
    group_count = c_send[0]
    for r in range(1, MEMBERS):
        group_count = group_count + c_recv[r]
    c_group[...] = group_count

    for h in (0, 1):
        z_send[h, 0, 3] = reduce_rows(0, h)
        forward(h, 0, 3)
    cz_send[0, 3] = count_of(4)
    forward_count(0, 3)

    def step(p, way, k, joined):
        for h in (0, 1):
            z_send[h, way, k] = reduce_rows(p, h)

            @pl.when(joined)
            def _():
                z_send[h, way, k] += incoming(h, way, k + 1)

            forward(h, way, k)
        count_step(way, k, joined)

    def count_step(way, k, joined):
        cz_send[way, k] = count_of(-k - 1 if way else k + 1)

        @pl.when(joined)
        def _():
            cz_send[way, k] += incoming_count(way, k + 1)

        forward_count(way, k)

    def pair(i, carry):
        k = 2 - i
        for way in (0, 1):
            p = 1 + 2 * i + way
            first(p + AHEAD - 1, 0)
            step(p, way, k, way == 0 or i > 0)
        return carry

    lax.fori_loop(0, 2, pair, 0)

    first(7, 0)
    step(5, 0, 0, True)
    onehots = [onehot_of(6, h) for h in (0, 1)]
    for h in (0, 1):
        await_bytes(z_recv.at[h, 1, 1], z_rs.at[h, 1, 1])
    for q in range(PIECES):
        for h in (0, 1):
            at = (h, 1, 0, slice(None), columns(q))
            z_send[at] = reduce_piece(onehots[h], 6, h, q) + z_recv[h, 1, 1, :, columns(q)]
            push(z_send.at[at], z_recv.at[at], last_ss.at[h, q], last_rs.at[h, q], onward(h, 1))
    count_step(1, 0, True)

    onehots = [onehot_of(7, h) for h in (0, 1)]
    for q in range(PIECES):
        for h in (0, 1):
            own = reduce_piece(onehots[h], 7, h, q)
            if q == 0:
                await_bytes(z_recv.at[h, 0, 0], z_rs.at[h, 0, 0])
            own = own + z_recv[h, 0, 0, :, columns(q)]
            await_bytes(z_recv.at[h, 1, 0, :, columns(q)], last_rs.at[h, q])
            own = own + z_recv[h, 1, 0, :, columns(q)]
            total[h, :, :, columns(q)] = own.reshape(4, OWN, PIECE)
            at = y if h == 0 else x
            for i in range(1, 4):
                push(
                    total.at[h, (at + i) % 4, :, columns(q)], part_recv.at[h, i, :, columns(q)],
                    part_ss.at[h, q], part_rs.at[h, q], other(h, i),
                )
        if q == 0:
            c_last[...] = count_of(0) + incoming_count(0, 0) + incoming_count(1, 0)
            for i in range(1, NY):
                push(c_last, c_last_recv.at[i], c_ss.at[1], c_rs.at[1], other(0, i))

    inputs[4].wait()
    await_bytes(c_last_recv.at[pl.ds(1, NY - 1)], c_rs.at[1])
    block_count = c_last[...]
    for i in range(1, NY):
        block_count = block_count + c_last_recv[i]
    for j in range(8):
        count_ref[j : j + 1, :] = block_count[:, j * 8 : (j + 1) * 8].astype(I32)
    own_sub = lax.broadcasted_iota(I32, (OWN, 128), 0) + y * OWN
    own_lane = lax.broadcasted_iota(I32, (OWN, 128), 1)
    column = jnp.sum(jnp.where(own_sub == own_lane, block_count, 0.0), axis=1, keepdims=True)

    for q in range(PIECES):
        for h in (0, 1):
            at = y if h == 0 else x
            cols = pl.ds(h * HALF + q * PIECE, PIECE)
            await_bytes(part_recv.at[h, pl.ds(1, 3), :, columns(q)], part_rs.at[h, q])
            mine = total[h, at, :, columns(q)]
            for i in range(1, 4):
                mine = mine + part_recv[h, i, :, columns(q)]
            old = old_ref[pl.ds(y * 2, 2), :, cols].reshape(OWN, PIECE)
            fresh[:, :, cols] = ((mine + old) / (column + 1.0)).reshape(2, 8, PIECE)
            src = fresh.at[:, :, cols]
            dst = out_ref.at[pl.ds(y * 2, 2), :, cols]
            for i in range(1, NY):
                push(src, dst, gather_ss.at[h, q], gather_rs.at[h, q], other(0, i))
            pltpu.make_async_copy(src, dst, own_sem.at[h, q]).start()

    for h in (0, 1):
        for p in range(8):
            await_bytes(lab_send.at[h, p, pl.ds(1, MEMBERS - 1)], lab_ss.at[h, p])
            if p < LATE:
                await_bytes(send.at[h, p, pl.ds(1, MEMBERS - 1)], data_ss.at[h, p])
        for way in (0, 1):
            for k in range(way, 4 - way):
                await_bytes(z_send.at[h, way, k], z_ss.at[h, way, k])
        for q in range(PIECES):
            for p in (6, 7):
                await_bytes(send.at[h, p, pl.ds(1, MEMBERS - 1), :, columns(q)], late_ss.at[h, p - LATE, q])
            await_bytes(z_send.at[h, 1, 0, :, columns(q)], last_ss.at[h, q])
            await_bytes(part_recv.at[h, pl.ds(1, 3), :, columns(q)], part_ss.at[h, q])
            cols = pl.ds(h * HALF + q * PIECE, PIECE)
            await_bytes(out_ref.at[pl.ds(0, 6), :, cols], gather_ss.at[h, q])
            await_bytes(out_ref.at[pl.ds(0, 6), :, cols], gather_rs.at[h, q])
            await_bytes(out_ref.at[pl.ds(0, 2), :, cols], own_sem.at[h, q])
    await_bytes(c_recv.at[pl.ds(1, MEMBERS - 1)], c_ss.at[0])
    await_bytes(c_last_recv.at[pl.ds(1, NY - 1)], c_ss.at[1])
    for way in (0, 1):
        for k in range(4 - way):
            await_bytes(cz_send.at[way, k], cz_ss.at[way, k])


def per_device(pool_rows, sample_index, cluster_id, child_id, old_centroids):
    vmem = pl.BlockSpec(memory_space=pltpu.VMEM)
    dma = pltpu.SemaphoreType.DMA
    centroids, counts = pl.pallas_call(
        kernel,
        out_shape=(
            jax.ShapeDtypeStruct((8, 8, WIDTH), F32),
            jax.ShapeDtypeStruct((8, 8), I32),
        ),
        in_specs=[pl.BlockSpec(memory_space=pltpu.HBM)] * 5,
        out_specs=(pl.BlockSpec(memory_space=pl.ANY), vmem),
        scratch_shapes=[
            pltpu.VMEM((ROWS, WIDTH), BF16),
            pltpu.VMEM((1, ROWS), I32),
            pltpu.VMEM((1, ROWS), I32),
            pltpu.VMEM((1, ROWS), I32),
            pltpu.VMEM((8, 8, WIDTH), F32),
            pltpu.VMEM((2, 1, ROWS), I32),
            pltpu.VMEM((ROWS, 128), BF16),
            pltpu.VMEM((2, 8, MEMBERS, SLOTS, HALF), BF16),
            pltpu.VMEM((2, 8, MEMBERS, SLOTS, HALF), BF16),
            pltpu.VMEM((2, 8, MEMBERS, 1, BLOCK), I32),
            pltpu.VMEM((2, 8, MEMBERS, 1, BLOCK), I32),
            pltpu.VMEM((2, 2, 4, SEGS, HALF), F32),
            pltpu.VMEM((2, 2, 4, SEGS, HALF), F32),
            pltpu.VMEM((2, 4, OWN, HALF), F32),
            pltpu.VMEM((2, 4, OWN, HALF), F32),
            pltpu.VMEM((2, 8, WIDTH), F32),
            pltpu.VMEM((MEMBERS, NZ, 128), F32),
            pltpu.VMEM((MEMBERS, NZ, 128), F32),
            pltpu.VMEM((NZ, 128), F32),
            pltpu.VMEM((2, 4, 1, 128), F32),
            pltpu.VMEM((2, 4, 1, 128), F32),
            pltpu.VMEM((1, 128), F32),
            pltpu.VMEM((NY, 1, 128), F32),
            dma((5,)), dma((2, 8)), dma((2, 8)), dma((2, 8)), dma((2, 8)),
            dma((2, 2, 4)), dma((2, 2, 4)), dma((2, PIECES)), dma((2, PIECES)),
            dma((2, PIECES)), dma((2, PIECES)), dma((2,)), dma((2,)), dma((2, 4)), dma((2, 4)),
            dma((2, PIECES)), dma((2, 2, PIECES)), dma((2, 2, PIECES)),
            dma((2, PIECES)), dma((2, PIECES)),
        ],
        compiler_params=pltpu.CompilerParams(
            collective_id=0, has_side_effects=True, vmem_limit_bytes=48 << 20
        ),
    )(
        *[
            pltpu.with_memory_space_constraint(a, pltpu.HBM)
            for a in (
                pool_rows,
                sample_index.reshape(1, ROWS),
                cluster_id.reshape(1, ROWS),
                child_id.reshape(1, ROWS),
                old_centroids,
            )
        ]
    )
    return centroids, counts


def solution(mesh):
    placed = (
        P(("grp", "dev"), None),
        P(("grp", "dev")),
        P(("grp", "dev")),
        P(("grp", "dev")),
        P("dev", None, None),
    )
    return jax.shard_map(
        per_device,
        mesh=mesh,
        in_specs=placed,
        out_specs=(P("dev", None, None), P("dev", None)),
        check_vma=False,
    )
```

time: 62.9 us -> 51.5 us (0.82)
  Pallas kernels: 56.1 us -> 49.1 us
  local copies, waits for them, and re-layouts: 5.89 us -> 1.3 us
    pallas_call x1, Pallas kernels: 56.1 us -> 49.1 us  [per_device(): pl.pallas_call(kernel, out_shape=(jax.ShapeDtypeStruct((8, 8, WIDTH), F32...]
    unnamed x12 -> x2, local copies, waits for them, and re-layouts: 5.89 us -> 1.3 us
where the time goes in v2:
time: 51.5 us; the launch traced here: 51 us
  Pallas kernels  49.1 us (95%)
  local copies, waits for them, and re-layouts  1.3 us (3%)
  between operations  0.64 us (1%)
    pallas_call x1, Pallas kernels, per_device(): pl.pallas_call(kernel, out_shape=(jax.ShapeDtypeStruct((8, 8, WIDTH), F32...  49.1 us
    unnamed x2, local copies, waits for them, and re-layouts  1.3 us

profile of v2, /device:TPU:1, one launch (start us, length us, event | category | flops | bytes accessed | tf_op | source)
XLA Modules:
  0.0 51.0 jit_solution(2527163078463181508)
XLA Ops:
  0.6 49.1 %shard_map.68 = (f32[8,8,1024]{2,1,0:T(8,128)S(1)}, s32[8,8]{1,0:T(8,128)S(1)}) custom-call(bf16[1024,1024]{1,0:T(8,128)(2,1)} %pool_hbm.1, s32[1,1024]{1,0:T(1,128)} %bitcast.3, s32[1,1024]{1,0:T(1,128)} %bitcast.4, s32[1,1024]{1,0:T(1,128)} %bitcast.5, f32[8,8,1024]{2,1,0:T(8,128)} %old_hbm.1), custom_call_target="tpu_custom_call" | custom-call | tf_op jit(solution)/shard_map/pallas_call | solution.py:372
  49.7 0.7 %copy.9 = f32[8,8,1024]{2,1,0:T(8,128)} copy(f32[8,8,1024]{2,1,0:T(8,128)S(1)} %get-tuple-element.4) | data formatting | bytes 524288
  50.4 0.6 %copy.10 = s32[8,8]{1,0:T(8,128)} copy(s32[8,8]{1,0:T(8,128)S(1)} %get-tuple-element.5) | data formatting | bytes 512

commit v3 on v2

--- a/solution.py
+++ b/solution.py
@@ -81,10 +81,15 @@
     cluster, child = cluster_ref[...], child_ref[...]
     index = index_ref[...] & (ROWS - 1)
     cx, cz, cc, cj = cluster >> 7, (cluster >> 4) & 7, (cluster >> 3) & 1, cluster & 7
+
+    def position(steps):
+        near = jnp.where(steps < 4, 8 - 2 * steps, 2 * steps - 9)
+        return jnp.where(steps == 0, 7, jnp.where(steps == 4, 0, near))
+
     zr = (cz - z + NZ) & (NZ - 1)
-    pos_x = jnp.where(zr >= 4, 2 * (zr - 4), 7 - 2 * zr)
+    pos_x = position(zr)
     zr = (NZ - zr) & (NZ - 1)
-    pos_y = jnp.where(zr >= 4, 2 * (zr - 4), 7 - 2 * zr)
+    pos_y = position(zr)
     rx = (cx * NC + cc - (x * NC + c) + MEMBERS) & (MEMBERS - 1)
     ry = ((cj >> 1) * NC + cc - (y * NC + c) + MEMBERS) & (MEMBERS - 1)
     label_x = cj * 8 + child
@@ -144,14 +149,14 @@
         return pl.ds(q * PIECE, PIECE)
 
     def dispatch(p, h):
-        for r in range(1, MEMBERS):
+        for r in (2, 6, 4, 3, 7, 5, 1):
             to = member(h, r)
             push(lab_send.at[h, p, r], lab_recv.at[h, p, r], lab_ss.at[h, p], lab_rs.at[h, p], to)
             push(send.at[h, p, r], recv.at[h, p, r], data_ss.at[h, p], data_rs.at[h, p], to)
 
     def dispatch_pieces(p, h):
         for q in range(PIECES):
-            for r in range(1, MEMBERS):
+            for r in (2, 6, 4, 3, 7, 5, 1):
                 to = member(h, r)
                 if q == 0:
                     push(lab_send.at[h, p, r], lab_recv.at[h, p, r], lab_ss.at[h, p], lab_rs.at[h, p], to)
@@ -274,8 +279,8 @@
 
     def pair(i, carry):
         k = 2 - i
-        for way in (0, 1):
-            p = 1 + 2 * i + way
+        for way in (1, 0):
+            p = 2 + 2 * i - way
             first(p + AHEAD - 1, 0)
             step(p, way, k, way == 0 or i > 0)
         return carry
@@ -283,26 +288,26 @@
     lax.fori_loop(0, 2, pair, 0)
 
     first(7, 0)
-    step(5, 0, 0, True)
+    step(5, 1, 0, True)
     onehots = [onehot_of(6, h) for h in (0, 1)]
     for h in (0, 1):
-        await_bytes(z_recv.at[h, 1, 1], z_rs.at[h, 1, 1])
+        await_bytes(z_recv.at[h, 0, 1], z_rs.at[h, 0, 1])
     for q in range(PIECES):
         for h in (0, 1):
-            at = (h, 1, 0, slice(None), columns(q))
-            z_send[at] = reduce_piece(onehots[h], 6, h, q) + z_recv[h, 1, 1, :, columns(q)]
-            push(z_send.at[at], z_recv.at[at], last_ss.at[h, q], last_rs.at[h, q], onward(h, 1))
-    count_step(1, 0, True)
+            at = (h, 0, 0, slice(None), columns(q))
+            z_send[at] = reduce_piece(onehots[h], 6, h, q) + z_recv[h, 0, 1, :, columns(q)]
+            push(z_send.at[at], z_recv.at[at], last_ss.at[h, q], last_rs.at[h, q], onward(h, 0))
+    count_step(0, 0, True)
 
     onehots = [onehot_of(7, h) for h in (0, 1)]
     for q in range(PIECES):
         for h in (0, 1):
             own = reduce_piece(onehots[h], 7, h, q)
             if q == 0:
-                await_bytes(z_recv.at[h, 0, 0], z_rs.at[h, 0, 0])
+                await_bytes(z_recv.at[h, 1, 0], z_rs.at[h, 1, 0])
+            own = own + z_recv[h, 1, 0, :, columns(q)]
+            await_bytes(z_recv.at[h, 0, 0, :, columns(q)], last_rs.at[h, q])
             own = own + z_recv[h, 0, 0, :, columns(q)]
-            await_bytes(z_recv.at[h, 1, 0, :, columns(q)], last_rs.at[h, q])
-            own = own + z_recv[h, 1, 0, :, columns(q)]
             total[h, :, :, columns(q)] = own.reshape(4, OWN, PIECE)
             at = y if h == 0 else x
             for i in range(1, 4):
@@ -348,12 +353,12 @@
             if p < LATE:
                 await_bytes(send.at[h, p, pl.ds(1, MEMBERS - 1)], data_ss.at[h, p])
         for way in (0, 1):
-            for k in range(way, 4 - way):
+            for k in range(1 - way, 4 - way):
                 await_bytes(z_send.at[h, way, k], z_ss.at[h, way, k])
         for q in range(PIECES):
             for p in (6, 7):
                 await_bytes(send.at[h, p, pl.ds(1, MEMBERS - 1), :, columns(q)], late_ss.at[h, p - LATE, q])
-            await_bytes(z_send.at[h, 1, 0, :, columns(q)], last_ss.at[h, q])
+            await_bytes(z_send.at[h, 0, 0, :, columns(q)], last_ss.at[h, q])
             await_bytes(part_recv.at[h, pl.ds(1, 3), :, columns(q)], part_ss.at[h, q])
             cols = pl.ds(h * HALF + q * PIECE, PIECE)
             await_bytes(out_ref.at[pl.ds(0, 6), :, cols], gather_ss.at[h, q])

time: 51.5 us -> 50.1 us (0.973)
  Pallas kernels: 49.1 us -> 48 us
    pallas_call x1, Pallas kernels: 49.1 us -> 48 us  [per_device(): pl.pallas_call(kernel, out_shape=(jax.ShapeDtypeStruct((8, 8, WIDTH), F32...]
where the time goes in v3:
time: 50.1 us; the launch traced here: 50 us
  Pallas kernels  48 us (96%)
  local copies, waits for them, and re-layouts  1.3 us (3%)
  between operations  0.64 us (1%)
    pallas_call x1, Pallas kernels, per_device(): pl.pallas_call(kernel, out_shape=(jax.ShapeDtypeStruct((8, 8, WIDTH), F32...  48 us
    unnamed x2, local copies, waits for them, and re-layouts  1.3 us

profile of v3, /device:TPU:1, one launch (start us, length us, event | category | flops | bytes accessed | tf_op | source)
XLA Modules:
  0.0 50.0 jit_solution(14310948557315655732)
XLA Ops:
  0.6 48.0 %shard_map.68 = (f32[8,8,1024]{2,1,0:T(8,128)S(1)}, s32[8,8]{1,0:T(8,128)S(1)}) custom-call(bf16[1024,1024]{1,0:T(8,128)(2,1)} %pool_hbm.1, s32[1,1024]{1,0:T(1,128)} %bitcast.3, s32[1,1024]{1,0:T(1,128)} %bitcast.4, s32[1,1024]{1,0:T(1,128)} %bitcast.5, f32[8,8,1024]{2,1,0:T(8,128)} %old_hbm.1), custom_call_target="tpu_custom_call" | custom-call | tf_op jit(solution)/shard_map/pallas_call | solution.py:377
  48.7 0.7 %copy.9 = f32[8,8,1024]{2,1,0:T(8,128)} copy(f32[8,8,1024]{2,1,0:T(8,128)S(1)} %get-tuple-element.4) | data formatting | bytes 524288
  49.4 0.6 %copy.10 = s32[8,8]{1,0:T(8,128)} copy(s32[8,8]{1,0:T(8,128)S(1)} %get-tuple-element.5) | data formatting | bytes 512

commit v4 on v3

--- a/solution.py
+++ b/solution.py
@@ -369,6 +369,17 @@
     for way in (0, 1):
         for k in range(4 - way):
             await_bytes(cz_send.at[way, k], cz_ss.at[way, k])
+
+
+def finish(centroids, counts, centroids_out, counts_out, sems):
+    copies = [
+        pltpu.make_async_copy(centroids, centroids_out, sems.at[0]),
+        pltpu.make_async_copy(counts, counts_out, sems.at[1]),
+    ]
+    for copy in copies:
+        copy.start()
+    for copy in copies:
+        copy.wait()
 
 
 def per_device(pool_rows, sample_index, cluster_id, child_id, old_centroids):
@@ -427,7 +438,16 @@
             )
         ]
     )
-    return centroids, counts
+    return pl.pallas_call(
+        finish,
+        out_shape=(
+            jax.ShapeDtypeStruct((8, 8, WIDTH), F32),
+            jax.ShapeDtypeStruct((8, 8), I32),
+        ),
+        in_specs=[vmem] * 2,
+        out_specs=(pl.BlockSpec(memory_space=pltpu.HBM),) * 2,
+        scratch_shapes=[dma((2,))],
+    )(*[pltpu.with_memory_space_constraint(a, pltpu.VMEM) for a in (centroids, counts)])
 
 
 def solution(mesh):

time: 50.1 us -> 49.5 us (0.988)
  local copies, waits for them, and re-layouts: 1.3 us -> 0 us
  Pallas kernels: 48 us -> 48.8 us
    unnamed x2 -> x0, local copies, waits for them, and re-layouts: 1.3 us -> none
    pallas_call x0 -> x1, Pallas kernels: none -> 0.72 us  [per_device(): pl.pallas_call(finish, out_shape=(jax.ShapeDtypeStruct((8, 8, WIDTH), F32...]
where the time goes in v4:
time: 49.5 us; the launch traced here: 49.4 us
  Pallas kernels  48.8 us (99%)
  between operations  0.64 us (1%)
    pallas_call x1, Pallas kernels, per_device(): pl.pallas_call(kernel, out_shape=(jax.ShapeDtypeStruct((8, 8, WIDTH), F32...  48 us

profile of v4, /device:TPU:1, one launch (start us, length us, event | category | flops | bytes accessed | tf_op | source)
XLA Modules:
  0.0 49.4 jit_solution(18361406729628368532)
XLA Ops:
  0.6 48.0 %shard_map.68 = (f32[8,8,1024]{2,1,0:T(8,128)S(1)}, s32[8,8]{1,0:T(8,128)S(1)}) custom-call(bf16[1024,1024]{1,0:T(8,128)(2,1)} %pool_hbm.1, s32[1,1024]{1,0:T(1,128)} %bitcast.3, s32[1,1024]{1,0:T(1,128)} %bitcast.4, s32[1,1024]{1,0:T(1,128)} %bitcast.5, f32[8,8,1024]{2,1,0:T(8,128)} %old_hbm.1), custom_call_target="tpu_custom_call" | custom-call | tf_op jit(solution)/shard_map/pallas_call | solution.py:388
  48.7 0.7 %shard_map.69 = (f32[8,8,1024]{2,1,0:T(8,128)}, s32[8,8]{1,0:T(8,128)}) custom-call(f32[8,8,1024]{2,1,0:T(8,128)S(1)} %get-tuple-element.4.centroids, s32[8,8]{1,0:T(8,128)S(1)} %get-tuple-element.5.counts), custom_call_target="tpu_custom_call" | custom-call | tf_op jit(solution)/shard_map/pallas_call | solution.py:441

commit v5 on v4

--- a/solution.py
+++ b/solution.py
@@ -125,7 +125,7 @@
 
     sub_block = lax.broadcasted_iota(I32, (BLOCK, ROWS), 0)
     lane_block = lax.broadcasted_iota(I32, (BLOCK, ROWS), 1)
-    lab_lane = lax.broadcasted_iota(I32, (1, BLOCK), 1)
+    lab_lane = lax.broadcasted_iota(I32, (1, BLOCK // 2), 1)
 
     def place(p, h):
         pick = jnp.where(sub_block == slot_ref[h] - p * BLOCK, 1.0, 0.0).astype(BF16)
@@ -139,7 +139,8 @@
         recv[h, p, 0] = rows[:SLOTS]
         send[h, p, pl.ds(1, MEMBERS - 1)] = rows[SLOTS:].reshape(MEMBERS - 1, SLOTS, HALF)
         for r in range(MEMBERS):
-            mine = jnp.where((lab_lane >> 5) == r, labels, 0)
+            half = labels[:, (r // 4) * 128 : (r // 4 + 1) * 128]
+            mine = jnp.where((lab_lane >> 5) == r % 4, half, 0)
             if r == 0:
                 lab_recv[h, p, 0] = mine
             else:
@@ -170,9 +171,10 @@
 
     def onehot_of(p, h):
         await_bytes(lab_recv.at[h, p, pl.ds(1, MEMBERS - 1)], lab_rs.at[h, p])
-        labels = lab_recv[h, p, 0]
-        for r in range(1, MEMBERS):
-            labels = labels + lab_recv[h, p, r]
+        low, high = lab_recv[h, p, 0], lab_recv[h, p, 4]
+        for r in range(1, 4):
+            low, high = low + lab_recv[h, p, r], high + lab_recv[h, p, 4 + r]
+        labels = jnp.concatenate([low, high], axis=1)
         return jnp.where(seg == labels, 1.0, 0.0).astype(BF16)
 
     def reduce_rows(p, h):
@@ -403,8 +405,8 @@
             pltpu.VMEM((ROWS, 128), BF16),
             pltpu.VMEM((2, 8, MEMBERS, SLOTS, HALF), BF16),
             pltpu.VMEM((2, 8, MEMBERS, SLOTS, HALF), BF16),
-            pltpu.VMEM((2, 8, MEMBERS, 1, BLOCK), I32),
-            pltpu.VMEM((2, 8, MEMBERS, 1, BLOCK), I32),
+            pltpu.VMEM((2, 8, MEMBERS, 1, BLOCK // 2), I32),
+            pltpu.VMEM((2, 8, MEMBERS, 1, BLOCK // 2), I32),
             pltpu.VMEM((2, 2, 4, SEGS, HALF), F32),
             pltpu.VMEM((2, 2, 4, SEGS, HALF), F32),
             pltpu.VMEM((2, 4, OWN, HALF), F32),

time: 49.5 us -> 49.6 us (level)
  no operation moved by 1% of the time
where the time goes in v5:
time: 49.6 us; the launch traced here: 49.4 us
  Pallas kernels  48.8 us (98%)
  between operations  0.64 us (1%)
    pallas_call x1, Pallas kernels, per_device(): pl.pallas_call(kernel, out_shape=(jax.ShapeDtypeStruct((8, 8, WIDTH), F32...  48.1 us

profile of v5, /device:TPU:1, one launch (start us, length us, event | category | flops | bytes accessed | tf_op | source)
XLA Modules:
  0.0 49.4 jit_solution(7256358793484060286)
XLA Ops:
  0.6 48.1 %shard_map.68 = (f32[8,8,1024]{2,1,0:T(8,128)S(1)}, s32[8,8]{1,0:T(8,128)S(1)}) custom-call(bf16[1024,1024]{1,0:T(8,128)(2,1)} %pool_hbm.1, s32[1,1024]{1,0:T(1,128)} %bitcast.3, s32[1,1024]{1,0:T(1,128)} %bitcast.4, s32[1,1024]{1,0:T(1,128)} %bitcast.5, f32[8,8,1024]{2,1,0:T(8,128)} %old_hbm.1), custom_call_target="tpu_custom_call" | custom-call | tf_op jit(solution)/shard_map/pallas_call | solution.py:390
  48.7 0.7 %shard_map.69 = (f32[8,8,1024]{2,1,0:T(8,128)}, s32[8,8]{1,0:T(8,128)}) custom-call(f32[8,8,1024]{2,1,0:T(8,128)S(1)} %get-tuple-element.4.centroids, s32[8,8]{1,0:T(8,128)S(1)} %get-tuple-element.5.counts), custom_call_target="tpu_custom_call" | custom-call | tf_op jit(solution)/shard_map/pallas_call | solution.py:443
